TPU v7x, 512 devices: a whole 4x8x8 slice. The times are simulated.
512 devices in a mesh: seq: 128 (over z, y, core), head: 4 (over x).
Axes of the slice: x: 4, y: 8, z: 8, core: 2. Of those that a mesh axis runs over, the one named last changes fastest.
Arguments:
- q_nope: bfloat16 [4, 64, 128], P(None, 'head'), may hold values from -5 to 5
- q_rope: bfloat16 [4, 64, 64], P(None, 'head'), may hold values from -16 to 16
- w_key_up: bfloat16 [64, 128, 512], P('head'), may hold values from -0.5 to 0.5
- w_value_up: bfloat16 [64, 512, 128], P('head'), may hold values from -0.25 to 0.25
- latent_cache: bfloat16 [8192, 64, 576], P('seq'), may hold values from -34 to 34
- page_scale: float32 [8192], P('seq'), may hold values from 0.25 to 2, as said below
- block_table: int32 [4, 2048], P(None, 'seq'), may hold values from 0 to 63, as said below
- lengths: int32 [4], replicated, may hold values from 1 to 131072, 327680 in all
Outputs:
- attn_out: bfloat16 [4, 8192], P('head', 'seq')
Inputs may be any that keep to these rules, and one draw needn't show every extreme that they name: `block_table`: each entry is the number of a page within its pool; for each index of seq, the entries of its 16 page columns over all requests name every page of its pool exactly once. `page_scale`: every page scale is positive. `lengths`: each request has at least one cached position and at most 131072; the longest has exactly 131072.
All inputs are finite; a program needn't handle non-finite values.
Results may differ from a plain program's by a relative error of at most 0.0095.
Values may be sent and summed in bfloat16 or wider, within the bound.
A program may use at most 64 MiB of HBM per device.

v0:
```python
import jax
import jax.numpy as jnp
from jax import lax
from jax.sharding import Mesh
from jax.sharding import PartitionSpec as P

ROPE = 64
NOPE = 128
SEQ = ("seq_0", "seq_1", "seq_2")


floor_score = -1e30


def collected_together(array, axis):
    leaves = jax.tree.leaves(array)
    order = sorted(range(len(leaves)), key=lambda k: -leaves[k].size)
    width = (1, *leaves[order[0]].shape)[-1]
    lines = [
        jnp.pad(leaves[k].reshape(-1), (0, -leaves[k].size % width)).reshape(-1, width)
        for k in order
    ]
    both, at, found = (lax.all_gather(jnp.concatenate(lines), axis), 0, {})
    for k, line in zip(order, lines):
        section = both[:, at : at + len(line)].reshape(len(both), -1)
        found[k] = section[:, : leaves[k].size].reshape(-1, *leaves[k].shape)
        at += len(line)
    numbers = iter(range(len(leaves)))
    return jax.tree.map(lambda _: found[next(numbers)], array)


def joined_all(array, axes, combine):
    for axis in axes:
        pieces = collected_together(array, axis)
        array = jax.tree.map(lambda part: part[0], pieces)
        for k in range(1, lax.axis_size(axis)):
            array = combine(array, jax.tree.map(lambda part: part[k], pieces))
    return array


def combine(former, latter):
    maximum = jnp.maximum(former[0], latter[0])
    factor_one = jnp.exp(former[0] - maximum)
    factor_two = jnp.exp(latter[0] - maximum)
    denominator = former[1] * factor_one + latter[1] * factor_two
    weighted = former[2] * factor_one[..., None] + latter[2] * factor_two[..., None]
    return (maximum, denominator, weighted)


def shards(q_nope, q_rope, w_key_up, w_value_up, latent_cache, page_scale, block_table, lengths):
    softmax_scale = (NOPE + ROPE) ** (-0.5)
    batch_rows, window = block_table.shape
    page_len = latent_cache.shape[1]
    ctx_local = window * page_len
    lat_width = latent_cache.shape[2] - q_rope.shape[2]
    value_up = w_value_up.astype(jnp.float32)
    q_latent = jnp.einsum(
        "bhn,hnl->bhl", q_nope, w_key_up, preferred_element_type=jnp.float32
    ).astype(jnp.bfloat16)
    cache_rows = latent_cache[block_table].reshape(batch_rows, ctx_local, latent_cache.shape[2])
    latent_rows = cache_rows[:, :, :lat_width]
    rope_rows = cache_rows[:, :, lat_width:]
    scale_rows = jnp.repeat(page_scale[block_table], page_len, axis=1)
    raw_scores = jnp.einsum(
        "bhl,btl->bht", q_latent, latent_rows, preferred_element_type=jnp.float32
    )
    raw_scores = raw_scores + jnp.einsum(
        "bhr,btr->bht", q_rope, rope_rows, preferred_element_type=jnp.float32
    )
    positions = lax.axis_index(SEQ) * ctx_local + jnp.arange(ctx_local, dtype=jnp.int32)
    usable = (positions[None, :] < lengths[:, None])[:, None, :]
    scores = jnp.where(usable, raw_scores * (scale_rows * softmax_scale)[:, None, :], floor_score)
    local_peak = jnp.max(scores, axis=2)
    weights = jnp.where(usable, jnp.exp(scores - local_peak[..., None]), 0.0)
    denominator = jnp.sum(weights, axis=2)
    probabilities = (weights * scale_rows[:, None, :]).astype(jnp.bfloat16)
    weighted = jnp.einsum(
        "bht,btl->bhl", probabilities, latent_rows, preferred_element_type=jnp.float32
    )
    carried = jnp.einsum("bhl,hlv->bhv", weighted, value_up, precision=lax.Precision.HIGHEST)
    denominator, carried = (denominator, carried)
    merged = joined_all((local_peak, denominator, carried), SEQ, combine)
    denominator, carried = (merged[1], merged[2])
    projected = carried / denominator[..., None]
    flattened = projected.reshape(batch_rows, projected.shape[1] * projected.shape[2]).astype(
        jnp.bfloat16
    )
    regrouped = lax.all_to_all(flattened, "head", split_axis=0, concat_axis=1, tiled=True)
    column_width = regrouped.shape[1] // lax.axis_size(SEQ)
    return lax.dynamic_slice_in_dim(regrouped, lax.axis_index(SEQ) * column_width, column_width, 1)


def solution(mesh):
    split = Mesh(
        mesh.devices.reshape(8, 8, 2, mesh.shape["head"]), ("seq_0", "seq_1", "seq_2", "head")
    )
    return jax.shard_map(
        shards,
        mesh=split,
        in_specs=(
            P(None, "head", None),
            P(None, "head", None),
            P("head", None, None),
            P("head", None, None),
            P(SEQ, None, None),
            P(SEQ),
            P(None, SEQ),
            P(),
        ),
        out_specs=P("head", SEQ),
        check_vma=False,
    )
```

profile of v0, /device:TPU:1, one launch (start us, length us, event | category | flops | bytes accessed | tf_op | source)
XLA Modules:
  0.0 89.6 jit_solution(12509337959068118223)
XLA Ops:
  0.0 0.8 compare_select_fusion
  0.8 0.1 reshape.1012
  0.9 1.4 %gather_fusion.1 = f32[64]{0:T(128)S(1)} fusion(f32[64]{0:T(128)} %param.13, s32[1024]{0:T(1024)S(1)} %pad_clamp_fusion), kind=kCustom, calls=%fused_computation.1 | custom fusion | bytes 768 | tf_op jit(solution)/shard_map/gather | solution.py:63
  2.4 0.1 reshape.1019
  2.5 0.1 reshape.994
  2.6 6.0 %gather_fusion = bf16[64,64,576]{2,1,0:T(8,128)(2,1)} fusion(bf16[64,64,576]{2,1,0:T(8,128)(2,1)} %param.12, s32[1024]{0:T(1024)S(1)} %pad_clamp_fusion), kind=kCustom, calls=%fused_computation | custom fusion | bytes 9437440 | tf_op jit(solution)/shard_map/gather | solution.py:60
  8.6 0.1 broadcast_compare_fusion
  8.7 0.4 fusion.7
  9.1 3.6 %fusion.2 = f32[4,16,1024]{2,1,0:T(8,128)S(1)} fusion(bf16[4,1024,576]{2,1,0:T(8,128)(2,1)} %bitcast.471, bf16[4,16,512]{2,0,1:T(4,128)(2,1)S(1)} %fusion.7), kind=kOutput, calls=%fused_computation.4 | convolution fusion | flops 67108864 | bytes 4521984 | tf_op jit(solution)/shard_map/bhl,btl->bht/dot_general | solution.py:64
  12.7 0.5 fusion.127
  13.2 0.7 fusion
  13.9 0.2 fusion.9
  14.1 0.1 reshape.996
  14.2 0.1 reshape.998
  14.3 2.6 %convolution_bitcast_fusion.1 = f32[4,16,128]{2,0,1:T(4,128)S(1)} fusion(bf16[16,512,128]{2,1,0:T(8,128)(2,1)} %param.11, f32[4,16,512]{2,1,0:T(8,128)S(1)} %fusion), kind=kOutput, calls=%fused_computation.12 | convolution fusion | flops 50331648 | bytes 2260992 | tf_op jit(solution)/shard_map/bhl,hlv->bhv/dot_general | solution.py:80
  16.9 26.0 %all-gather.3 = f32[8,66,128]{2,1,0:T(8,128)S(1)} all-gather(f32[1,66,128]{2,1,0:T(8,128)S(1)} %maximum_bitcast_fusion), channel_id=2, replica_groups=mesh['seq_0'=8,'seq_1'=8,'seq_2'=2,'head'=4] {'seq_0'}, dimensions={0}, use_global_device_ids=true | all-gather | bytes 304128 | tf_op jit(solution)/shard_map/all_gather | solution.py:23
  43.0 0.2 fusion.38
  43.2 20.2 %all-gather.4 = f32[8,66,128]{2,1,0:T(8,128)S(1)} all-gather(f32[1,66,128]{2,1,0:T(8,128)S(1)} %maximum_bitcast_fusion.1), channel_id=3, replica_groups=mesh['seq_0'=8,'seq_1'=8,'seq_2'=2,'head'=4] {'seq_1'}, dimensions={0}, use_global_device_ids=true | all-gather | bytes 304128 | tf_op jit(solution)/shard_map/all_gather | solution.py:23
  63.5 0.2 fusion.17
  63.7 14.5 %all-gather.5 = f32[2,66,128]{2,1,0:T(8,128)S(1)} all-gather(f32[1,66,128]{2,1,0:T(8,128)S(1)} %maximum_bitcast_fusion.2), channel_id=4, replica_groups=mesh['seq_0'=8,'seq_1'=8,'seq_2'=2,'head'=4] {'seq_2'}, dimensions={0}, use_global_device_ids=true | all-gather | bytes 101376 | tf_op jit(solution)/shard_map/all_gather | solution.py:23
  78.3 0.1 squeeze.211
  78.3 0.1 squeeze.214
  78.4 0.1 squeeze.212
  78.5 0.1 squeeze.215
  78.6 0.1 div.18
  78.8 0.1 fusion.58
  78.9 0.5 broadcast.95
  79.4 0.7 reduce.16
  80.2 0.6 reshape.1065
  80.8 4.0 %all-to-all-start = ((bf16[4,2,1024]{2,1,0:T(2,128)(2,1)}), bf16[4,2,1024]{2,1,0:T(2,128)(2,1)S(1)}, u32[]{:S(2)}, u32[]{:S(2)}) async-start(bf16[4,2,1024]{2,1,0:T(2,128)(2,1)} %reshape.1065), calls=%async_computation | async-start | bytes 32768 | tf_op jit(solution)/shard_map/all_to_all | solution.py:88
  84.8 4.2 %all-to-all-done = bf16[4,2,1024]{2,1,0:T(2,128)(2,1)S(1)} async-done(((bf16[4,2,1024]{2,1,0:T(2,128)(2,1)}), bf16[4,2,1024]{2,1,0:T(2,128)(2,1)S(1)}, u32[]{:S(2)}, u32[]{:S(2)}) %all-to-all-start) | async-done | bytes 16416 | tf_op jit(solution)/shard_map/all_to_all | solution.py:88
  89.0 0.6 constant_dynamic-slice_fusion
  (37 shorter events, 0.5 us)
Async XLA Ops:
  0.0 8.7 %copy-start = (bf16[16,128,512]{2,1,0:T(8,128)(2,1)S(1)}, bf16[16,128,512]{2,1,0:T(8,128)(2,1)}, u32[]{:S(2)}) copy-start(bf16[16,128,512]{2,1,0:T(8,128)(2,1)} %param.10) | copy-start | bytes 6291460
  2.6 6.0 %copy-start.3 = (s32[4]{0:T(128)S(1)}, s32[4]{0:T(128)}, u32[]{:S(2)}) copy-start(s32[4]{0:T(128)} %param.15) | copy-start | bytes 52
  2.6 6.1 %copy-start.2 = (bf16[4,16,128]{2,1,0:T(8,128)(2,1)S(1)}, bf16[4,16,128]{2,1,0:T(8,128)(2,1)}, u32[]{:S(2)}) copy-start(bf16[4,16,128]{2,1,0:T(8,128)(2,1)} %param.8) | copy-start | bytes 49156
  8.6 4.1 %copy-start.1 = (bf16[64,64,576]{2,1,0:T(8,128)(2,1)S(1)}, bf16[64,64,576]{2,1,0:T(8,128)(2,1)}, u32[]{:S(2)}) copy-start(bf16[64,64,576]{2,1,0:T(8,128)(2,1)} %gather_fusion) | copy-start | bytes 14155780
  8.6 4.1 %copy-start.4 = (bf16[4,16,64]{2,1,0:T(8,128)(2,1)S(1)}, bf16[4,16,64]{2,1,0:T(8,128)(2,1)}, u32[]{:S(2)}) copy-start(bf16[4,16,64]{2,1,0:T(8,128)(2,1)} %param.9) | copy-start | bytes 24580
  80.8 8.2 %all-to-all-start = ((bf16[4,2,1024]{2,1,0:T(2,128)(2,1)}), bf16[4,2,1024]{2,1,0:T(2,128)(2,1)S(1)}, u32[]{:S(2)}, u32[]{:S(2)}) async-start(bf16[4,2,1024]{2,1,0:T(2,128)(2,1)} %reshape.1065), calls=%async_computation | async-start | bytes 32768 | tf_op jit(solution)/shard_map/all_to_all | solution.py:88
where the time goes:
time: 89.9 us; the launch traced here: 89.6 us
  blocking collectives  60.7 us (68%)
  local copies, waits for them, and re-layouts  10.3 us (11%)
  matrix products  7.77 us (9%)
  waiting for transfers between devices  4.21 us (5%)
  starting transfers between devices  4.01 us (4%)
  other arithmetic  2.47 us (3%)
    all_gather x3, blocking collectives, collected_together(): both, at, found = (lax.all_gather(jnp.concatenate(lines), axis), 0, {})  60.7 us
    gather x1, local copies, waits for them, and re-layouts, shards(): latent_cache[block_table]  5.98 us
    all_to_all x1, waiting for transfers between devices, shards(): lax.all_to_all(flattened, 'head', split_axis=0, concat_axis=1, tiled=True)  4.21 us
    all_to_all x1, starting transfers between devices, shards(): lax.all_to_all(flattened, 'head', split_axis=0, concat_axis=1, tiled=True)  4.01 us
    dot_general x1, matrix products, shards(): jnp.einsum('bhl,btl->bht', q_latent, latent_rows, preferred_element_type=...  3.61 us
    dot_general x1, matrix products, shards(): jnp.einsum('bhl,hlv->bhv', weighted, value_up, precision=lax.Precision.HI...  2.58 us
  transfers between devices with their start and end apart: 1, of which 1 were waited for; matrix products, arithmetic and copies ran while one was open for 0% of the time, Pallas kernels for 0%

commit v1 on v0

v1 whole, which is shorter than its diff:
```python
import jax
import jax.numpy as jnp
from jax import lax
from jax.experimental import pallas as pl
from jax.experimental.pallas import tpu as pltpu
from jax.sharding import Mesh
from jax.sharding import PartitionSpec as P

SEQ = ("seq_0", "seq_1", "seq_2")
F32 = jnp.float32
BF16 = jnp.bfloat16
MESH_ID = pl.DeviceIdType.MESH

BATCH = 4
HEADS = 16
ROWS = BATCH * HEADS
LAT = 512
ROPE = 64
NOPE = 128
VDIM = 128
PAGE = 64
PAGES = 64
BLOCKS = 16
CHUNK = 8
CHUNKS = PAGES // CHUNK
SPAN = CHUNK * PAGE
GROUP = 16
NZ = 8
FLOOR = -1e30


def to_column(row, eye):
    return jnp.sum(jnp.where(eye, jnp.broadcast_to(row, eye.shape), 0.0), axis=1, keepdims=True)


def kernel(
    qn_hbm, qr_hbm, wk_hbm, wv_hbm, cache_hbm, ps_hbm, bt_hbm, len_hbm, out_ref,
    qn, qr, wk, wv, cache, ps, bt, ln, qs, qrs, ql, s_buf, vc,
    send_a, recv_a, send_b, recv_b,
    in_sem, cache_sem, a_send, a_recv, b_send, b_recv,
):
    z = lax.axis_index("seq_0")
    y = lax.axis_index("seq_1")
    c = lax.axis_index("seq_2")
    x = lax.axis_index("head")

    small = [
        pltpu.make_async_copy(src, dst, in_sem.at[k])
        for k, (src, dst) in enumerate(
            [(qn_hbm, qn), (qr_hbm, qr), (bt_hbm, bt), (len_hbm, ln), (ps_hbm, ps), (wk_hbm, wk), (wv_hbm, wv)]
        )
    ]
    pages = [
        pltpu.make_async_copy(
            cache_hbm.at[pl.ds(k * CHUNK, CHUNK)], cache.at[pl.ds(k * CHUNK, CHUNK)], cache_sem.at[k]
        )
        for k in range(CHUNKS)
    ]
    for copy in small[:6]:
        copy.start()
    for copy in pages:
        copy.start()
    small[6].start()

    mine = c * 8 + y
    target_z = 2 * x + c
    alone = z == target_z
    barrier = pltpu.get_barrier_semaphore()
    for o in range(1, GROUP):
        peer = lax.rem(mine + o, GROUP)
        pl.semaphore_signal(
            barrier, inc=1, device_id=(z, lax.rem(peer, 8), lax.div(peer, 8), x), device_id_type=MESH_ID
        )
    for k in range(NZ):
        is_self = jnp.logical_and(alone, z == k)

        @pl.when(jnp.logical_not(is_self))
        def _():
            pl.semaphore_signal(
                barrier, inc=1, device_id=(k, y, lax.rem(z, 2), lax.div(z, 2)), device_id_type=MESH_ID
            )

    for copy in small[:5]:
        copy.wait()
    column = lax.broadcasted_iota(jnp.int32, (PAGES, ROWS), 1)
    request = lax.rem(column, BATCH)
    first = ((z * 8 + y) * 2 + c) * (BLOCKS * PAGE)
    page_id = lax.broadcasted_iota(jnp.int32, (PAGES, BLOCKS), 0)
    block = lax.broadcasted_iota(jnp.int32, (PAGES, BLOCKS), 1)
    valid = jnp.zeros((PAGES, ROWS), F32)
    for b in range(BATCH):
        left = jnp.clip(ln[b] - first - block * PAGE, 0, PAGE).astype(F32)
        owned = jnp.where(jnp.broadcast_to(bt[b : b + 1, :], (PAGES, BLOCKS)) == page_id, left, 0.0)
        valid = jnp.where(request == b, jnp.sum(owned, axis=1, keepdims=True), valid)
    vc[...] = valid

    for b in range(BATCH):
        qs[pl.ds(b, HEADS, stride=BATCH), :] = qn[b].astype(F32)
        qrs[pl.ds(b, HEADS, stride=BATCH), :] = qr[b].astype(F32)
    q_rope = qrs[...].astype(BF16)
    small[5].wait()
    for h in range(HEADS):
        lhs = qs[pl.ds(16 * (h // 4), 16), :].astype(BF16)
        part = jnp.dot(lhs, wk[h], preferred_element_type=F32)
        at = 4 * (h % 4)
        ql[pl.ds(4 * h, 4), :] = part[at : at + 4]
    q_lat = ql[...].astype(BF16)

    contract = (((1,), (1,)), ((), ()))
    row_id = lax.broadcasted_iota(jnp.int32, (PAGE, ROWS), 0).astype(F32)
    peak = jnp.full((PAGE, ROWS), FLOOR, F32)
    for k in range(CHUNKS):
        pages[k].wait()
        lat_rows = cache[pl.ds(k * CHUNK, CHUNK), :, :LAT].reshape(SPAN, LAT)
        rope_rows = cache[pl.ds(k * CHUNK, CHUNK), :, LAT:].reshape(SPAN, ROPE)
        raw = lax.dot_general(lat_rows, q_lat, contract, preferred_element_type=F32)
        raw = raw + lax.dot_general(rope_rows, q_rope, contract, preferred_element_type=F32)
        for i in range(CHUNK):
            p = k * CHUNK + i
            scaled = raw[i * PAGE : (i + 1) * PAGE] * (ps[p] * (NOPE + ROPE) ** (-0.5))
            score = jnp.where(row_id < vc[pl.ds(p, 1), :], scaled, FLOOR)
            s_buf[pl.ds(p * PAGE, PAGE), :] = score
            peak = jnp.maximum(peak, score)
    peak = jnp.max(peak, axis=0, keepdims=True)
    floor = jnp.maximum(peak, -1e29)

    total = jnp.zeros((PAGE, ROWS), F32)
    latent = jnp.zeros((ROWS, LAT), F32)
    for k in range(CHUNKS):
        pieces = []
        for i in range(CHUNK):
            p = k * CHUNK + i
            weight = jnp.exp(s_buf[pl.ds(p * PAGE, PAGE), :] - floor)
            total = total + weight
            pieces.append(weight * ps[p])
        prob = jnp.concatenate(pieces, axis=0).T.astype(BF16)
        lat_rows = cache[pl.ds(k * CHUNK, CHUNK), :, :LAT].reshape(SPAN, LAT)
        latent = latent + jnp.dot(prob, lat_rows, preferred_element_type=F32)
    denominator = jnp.sum(total, axis=0, keepdims=True)

    eye = lax.broadcasted_iota(jnp.int32, (ROWS, ROWS), 0) == lax.broadcasted_iota(jnp.int32, (ROWS, ROWS), 1)
    some = denominator > 0.0
    safe = jnp.where(some, denominator, 1.0)
    level = to_column(jnp.where(some, floor + jnp.log(safe), FLOOR), eye)
    inverse = to_column(1.0 / safe, eye)
    level = jnp.broadcast_to(level, (ROWS, VDIM))
    latent = (latent * inverse).astype(BF16)

    small[6].wait()
    for h in range(HEADS):
        part = jnp.dot(latent[16 * (h // 4) : 16 * (h // 4) + 16], wv[h], preferred_element_type=F32)
        at = 4 * (h % 4)
        send_a[h, 0] = part[at : at + 4]
        send_a[h, 1] = level[4 * h : 4 * h + 4]

    pl.semaphore_wait(barrier, GROUP - 1 + NZ - jnp.where(alone, 1, 0))

    first_copies = []
    for o in range(1, GROUP):
        peer = lax.rem(mine + o, GROUP)
        copy = pltpu.make_async_remote_copy(
            src_ref=send_a.at[peer],
            dst_ref=recv_a.at[mine],
            send_sem=a_send.at[o],
            recv_sem=a_recv.at[mine],
            device_id=(z, lax.rem(peer, 8), lax.div(peer, 8), x),
            device_id_type=MESH_ID,
        )
        copy.start()
        first_copies.append(copy)
    recv_a[mine] = send_a[mine]
    for o in range(1, GROUP):
        peer = lax.rem(mine + o, GROUP)
        pltpu.make_async_remote_copy(
            src_ref=send_a.at[peer],
            dst_ref=recv_a.at[peer],
            send_sem=a_send.at[o],
            recv_sem=a_recv.at[peer],
            device_id=(z, lax.rem(peer, 8), lax.div(peer, 8), x),
            device_id_type=MESH_ID,
        ).wait_recv()
    levels = recv_a[:, 1]
    top = jnp.max(levels, axis=0)
    share = jnp.exp(levels - top[None])
    whole = jnp.sum(share, axis=0)
    send_b[:, 0] = (jnp.sum(share * recv_a[:, 0], axis=0) / whole).reshape(BATCH, 1, VDIM)
    send_b[:, 1] = (top + jnp.log(whole)).reshape(BATCH, 1, VDIM)

    def second(b, core):
        return pltpu.make_async_remote_copy(
            src_ref=send_b.at[b],
            dst_ref=recv_b.at[z],
            send_sem=b_send.at[2 * b + core],
            recv_sem=b_recv.at[z],
            device_id=(target_z, y, core, b),
            device_id_type=MESH_ID,
        )

    for b in range(BATCH):
        for core in range(2):
            is_self = jnp.logical_and(alone, jnp.logical_and(x == b, c == core))

            @pl.when(jnp.logical_not(is_self))
            def _():
                second(b, core).start()

    @pl.when(alone)
    def _():
        recv_b[z] = send_b[x]

    for k in range(NZ):

        @pl.when(jnp.logical_not(jnp.logical_and(alone, z == k)))
        def _():
            pltpu.make_async_remote_copy(
                src_ref=send_b.at[0],
                dst_ref=recv_b.at[k],
                send_sem=b_send.at[0],
                recv_sem=b_recv.at[k],
                device_id=(k, y, lax.rem(z, 2), lax.div(z, 2)),
                device_id_type=MESH_ID,
            ).wait_recv()

    levels = recv_b[:, 1]
    top = jnp.max(levels, axis=0)
    share = jnp.exp(levels - top[None])
    result = jnp.sum(share * recv_b[:, 0], axis=0) / jnp.sum(share, axis=0)
    out_ref[...] = jnp.where(c == 0, result[:, :64], result[:, 64:]).astype(BF16)

    for copy in first_copies:
        copy.wait_send()
    for b in range(BATCH):
        for core in range(2):
            is_self = jnp.logical_and(alone, jnp.logical_and(x == b, c == core))

            @pl.when(jnp.logical_not(is_self))
            def _():
                second(b, core).wait_send()


def shards(q_nope, q_rope, w_key_up, w_value_up, latent_cache, page_scale, block_table, lengths):
    hbm = pl.BlockSpec(memory_space=pl.ANY)
    dma = pltpu.SemaphoreType.DMA
    return pl.pallas_call(
        kernel,
        out_shape=jax.ShapeDtypeStruct((1, VDIM // 2), BF16),
        in_specs=[hbm] * 8,
        out_specs=pl.BlockSpec(memory_space=pltpu.VMEM),
        scratch_shapes=[
            pltpu.VMEM((BATCH, HEADS, NOPE), BF16),
            pltpu.VMEM((BATCH, HEADS, ROPE), BF16),
            pltpu.VMEM((HEADS, NOPE, LAT), BF16),
            pltpu.VMEM((HEADS, LAT, VDIM), BF16),
            pltpu.VMEM((PAGES, PAGE, LAT + ROPE), BF16),
            pltpu.SMEM((PAGES,), F32),
            pltpu.VMEM((BATCH, BLOCKS), jnp.int32),
            pltpu.SMEM((BATCH,), jnp.int32),
            pltpu.VMEM((ROWS, NOPE), F32),
            pltpu.VMEM((ROWS, ROPE), F32),
            pltpu.VMEM((ROWS, LAT), F32),
            pltpu.VMEM((PAGES * PAGE, ROWS), F32),
            pltpu.VMEM((PAGES, ROWS), F32),
            pltpu.VMEM((GROUP, 2, BATCH, VDIM), F32),
            pltpu.VMEM((GROUP, 2, BATCH, VDIM), F32),
            pltpu.VMEM((BATCH, 2, 1, VDIM), F32),
            pltpu.VMEM((NZ, 2, 1, VDIM), F32),
            dma((7,)),
            dma((CHUNKS,)),
            dma((GROUP,)),
            dma((GROUP,)),
            dma((2 * BATCH,)),
            dma((NZ,)),
        ],
        compiler_params=pltpu.CompilerParams(collective_id=0, has_side_effects=True),
        name="latent_decode",
    )(q_nope, q_rope, w_key_up, w_value_up, latent_cache, page_scale, block_table, lengths)


def solution(mesh):
    split = Mesh(
        mesh.devices.reshape(8, 8, 2, mesh.shape["head"]), ("seq_0", "seq_1", "seq_2", "head")
    )
    return jax.shard_map(
        shards,
        mesh=split,
        in_specs=(
            P(None, "head", None),
            P(None, "head", None),
            P("head", None, None),
            P("head", None, None),
            P(SEQ, None, None),
            P(SEQ),
            P(None, SEQ),
            P(),
        ),
        out_specs=P("head", SEQ),
        check_vma=False,
    )
```

time: 89.9 us -> 30.7 us (0.34)
  blocking collectives: 60.7 us -> 0 us
  Pallas kernels: 0 us -> 29.3 us
  local copies, waits for them, and re-layouts: 10.3 us -> 1.19 us
  matrix products: 7.77 us -> 0 us
  waiting for transfers between devices: 4.21 us -> 0 us
  starting transfers between devices: 4.01 us -> 0 us
  other arithmetic: 2.47 us -> 0 us
    all_gather x3 -> x0, blocking collectives: 60.7 us -> none  [collected_together(): both, at, found = (lax.all_gather(jnp.concatenate(lines), axis), 0, {})]
    pallas_call x0 -> x1, Pallas kernels: none -> 29.3 us  [shards(): pl.pallas_call(kernel, out_shape=jax.ShapeDtypeStruct((1, VDIM // 2), BF1...]
    dot_general x5 -> x0, matrix products: 7.77 us -> none  [the longest x1 3.61 us: shards(): jnp.einsum('bhl,btl->bht', q_latent, latent_rows, preferred_element_type=...]
    gather x3 -> x0, local copies, waits for them, and re-layouts: 7.5 us -> none  [the longest x1 5.98 us: shards(): latent_cache[block_table]]
    all_to_all x1 -> x0, waiting for transfers between devices: 4.21 us -> none  [shards(): lax.all_to_all(flattened, 'head', split_axis=0, concat_axis=1, tiled=True)]
    all_to_all x1 -> x0, starting transfers between devices: 4.01 us -> none  [shards(): lax.all_to_all(flattened, 'head', split_axis=0, concat_axis=1, tiled=True)]
  transfers between devices with their start and end apart: 1 -> 0, of which waited for: 1 -> 0; matrix products, arithmetic and copies ran while one was open for 0% -> 0% of each run, Pallas kernels for 0% -> 0%
where the time goes in v1:
time: 30.7 us; the launch traced here: 30.5 us
  Pallas kernels  29.3 us (95%)
  local copies, waits for them, and re-layouts  1.19 us (4%)
    pallas_call x1, Pallas kernels, shards(): pl.pallas_call(kernel, out_shape=jax.ShapeDtypeStruct((1, VDIM // 2), BF1...  29.3 us
    unnamed x1, local copies, waits for them, and re-layouts  1.19 us

profile of v1, /device:TPU:1, one launch (start us, length us, event | category | flops | bytes accessed | tf_op | source)
XLA Modules:
  0.0 30.5 jit_solution(6234605883624771383)
XLA Ops:
  0.0 29.3 %latent_decode.1 = bf16[1,64]{1,0:T(2,128)(2,1)} custom-call(bf16[4,16,128]{2,1,0:T(8,128)(2,1)} %qn_hbm.1, bf16[4,16,64]{2,1,0:T(8,128)(2,1)} %qr_hbm.1, bf16[16,128,512]{2,1,0:T(8,128)(2,1)} %wk_hbm.1, bf16[16,512,128]{2,1,0:T(8,128)(2,1)} %wv_hbm.1, bf16[64,64,576]{2,1,0:T(8,128)(2,1)} %cache_hbm.1, f32[64]{0:T(128)} %ps_hbm.1, s32[4,16]{1,0:T(4,128)} %bt_hbm.1, ...), custom_call_target="tpu_custom_call" | custom-call | tf_op jit(solution)/shard_map/latent_decode/pallas_call | solution.py:244
  29.4 1.2 %copy.10 = bf16[1,64]{1,0:T(2,128)(2,1)} copy(bf16[1,64]{1,0:T(2,128)(2,1)} %latent_decode.1) | data formatting | bytes 256

commit v2 on v1

v2 whole, which is shorter than its diff:
```python
import jax
import jax.numpy as jnp
from jax import lax
from jax.experimental import pallas as pl
from jax.experimental.pallas import tpu as pltpu
from jax.sharding import Mesh
from jax.sharding import PartitionSpec as P

SEQ = ("seq_0", "seq_1", "seq_2")
F32 = jnp.float32
BF16 = jnp.bfloat16
MESH_ID = pl.DeviceIdType.MESH

BATCH = 4
HEADS = 16
ROWS = BATCH * HEADS
LAT = 512
ROPE = 64
NOPE = 128
VDIM = 128
HALF = VDIM // 2
PAGE = 64
PAGES = 64
BLOCKS = 16
CHUNK = 8
CHUNKS = PAGES // CHUNK
SPAN = CHUNK * PAGE
PIECES = 4
PIECE = HEADS // PIECES
SOURCES = 128
FLOOR = -1e30


def to_column(row, eye):
    return jnp.sum(jnp.where(eye, jnp.broadcast_to(row, eye.shape), 0.0), axis=1, keepdims=True)


def kernel(
    qn_hbm, qr_hbm, wk_hbm, wv_hbm, cache_hbm, ps_hbm, bt_hbm, len_hbm, out_ref,
    qn, qr, wk, wv, cache, ps, bt, ln, qs, qrs, ql, s_buf, vc, send, recv,
    in_sem, wk_sem, cache_sem, send_sem, recv_sem,
):
    z = lax.axis_index("seq_0")
    y = lax.axis_index("seq_1")
    c = lax.axis_index("seq_2")
    x = lax.axis_index("head")

    small = [
        pltpu.make_async_copy(src, dst, in_sem.at[k])
        for k, (src, dst) in enumerate(
            [(qn_hbm, qn), (qr_hbm, qr), (bt_hbm, bt), (len_hbm, ln), (ps_hbm, ps), (wv_hbm, wv)]
        )
    ]
    keys = [
        pltpu.make_async_copy(
            wk_hbm.at[pl.ds(k * PIECE, PIECE)], wk.at[pl.ds(k * PIECE, PIECE)], wk_sem.at[k]
        )
        for k in range(PIECES)
    ]
    pages = [
        pltpu.make_async_copy(
            cache_hbm.at[pl.ds(k * CHUNK, CHUNK)], cache.at[pl.ds(k * CHUNK, CHUNK)], cache_sem.at[k]
        )
        for k in range(CHUNKS)
    ]
    for copy in small[:5] + keys + pages[:2]:
        copy.start()

    me = (z * 8 + y) * 2 + c
    plane = lax.div(z, 2)
    alone = plane == x
    barrier = pltpu.get_barrier_semaphore()
    for k in range(SOURCES):
        is_self = jnp.logical_and(alone, me == k)
        core = jnp.where(is_self, 1 - k % 2, k % 2)
        pl.semaphore_signal(
            barrier, inc=1, device_id=(k // 16, (k // 2) % 8, core, plane), device_id_type=MESH_ID
        )

    for copy in small[:5]:
        copy.wait()
    for b in range(BATCH):
        qs[pl.ds(b, HEADS, stride=BATCH), :] = qn[b].astype(F32)
        qrs[pl.ds(b, HEADS, stride=BATCH), :] = qr[b].astype(F32)
    q_rope = qrs[...].astype(BF16)

    column = lax.broadcasted_iota(jnp.int32, (PAGES, ROWS), 1)
    request = lax.rem(column, BATCH)
    first = me * (BLOCKS * PAGE)
    page_id = lax.broadcasted_iota(jnp.int32, (PAGES, BLOCKS), 0)
    block = lax.broadcasted_iota(jnp.int32, (PAGES, BLOCKS), 1)
    valid = jnp.zeros((PAGES, ROWS), F32)
    for b in range(BATCH):
        left = jnp.clip(ln[b] - first - block * PAGE, 0, PAGE).astype(F32)
        owned = jnp.where(jnp.broadcast_to(bt[b : b + 1, :], (PAGES, BLOCKS)) == page_id, left, 0.0)
        valid = jnp.where(request == b, jnp.sum(owned, axis=1, keepdims=True), valid)
    vc[...] = valid

    for k in range(PIECES):
        keys[k].wait()
        if 2 + k < CHUNKS:
            pages[2 + k].start()
        for h in range(k * PIECE, (k + 1) * PIECE):
            lhs = qs[pl.ds(16 * (h // 4), 16), :].astype(BF16)
            part = jnp.dot(lhs, wk[h], preferred_element_type=F32)
            at = 4 * (h % 4)
            ql[pl.ds(4 * h, 4), :] = part[at : at + 4]
    q_lat = ql[...].astype(BF16)

    contract = (((1,), (1,)), ((), ()))
    row_id = lax.broadcasted_iota(jnp.int32, (PAGE, ROWS), 0).astype(F32)
    peak = jnp.full((PAGE, ROWS), FLOOR, F32)
    for k in range(CHUNKS):
        pages[k].wait()
        if 2 + PIECES + k < CHUNKS:
            pages[2 + PIECES + k].start()
        elif 2 + PIECES + k == CHUNKS:
            small[5].start()
        lat_rows = cache[pl.ds(k * CHUNK, CHUNK), :, :LAT].reshape(SPAN, LAT)
        rope_rows = cache[pl.ds(k * CHUNK, CHUNK), :, LAT:].reshape(SPAN, ROPE)
        raw = lax.dot_general(lat_rows, q_lat, contract, preferred_element_type=F32)
        raw = raw + lax.dot_general(rope_rows, q_rope, contract, preferred_element_type=F32)
        for i in range(CHUNK):
            p = k * CHUNK + i
            scaled = raw[i * PAGE : (i + 1) * PAGE] * (ps[p] * (NOPE + ROPE) ** (-0.5))
            score = jnp.where(row_id < vc[pl.ds(p, 1), :], scaled, FLOOR)
            s_buf[pl.ds(p * PAGE, PAGE), :] = score
            peak = jnp.maximum(peak, score)
    peak = jnp.max(peak, axis=0, keepdims=True)
    floor = jnp.maximum(peak, -1e29)

    total = jnp.zeros((PAGE, ROWS), F32)
    latent = jnp.zeros((ROWS, LAT), F32)
    for k in range(CHUNKS):
        pieces = []
        for i in range(CHUNK):
            p = k * CHUNK + i
            weight = jnp.exp(s_buf[pl.ds(p * PAGE, PAGE), :] - floor)
            total = total + weight
            pieces.append(weight * ps[p])
        prob = jnp.concatenate(pieces, axis=0).T.astype(BF16)
        lat_rows = cache[pl.ds(k * CHUNK, CHUNK), :, :LAT].reshape(SPAN, LAT)
        latent = latent + jnp.dot(prob, lat_rows, preferred_element_type=F32)
    denominator = jnp.sum(total, axis=0, keepdims=True)

    eye = lax.broadcasted_iota(jnp.int32, (ROWS, ROWS), 0) == lax.broadcasted_iota(jnp.int32, (ROWS, ROWS), 1)
    some = denominator > 0.0
    safe = jnp.where(some, denominator, 1.0)
    level = to_column(jnp.where(some, floor + jnp.log(safe), FLOOR), eye)
    inverse = to_column(1.0 / safe, eye)
    level = jnp.broadcast_to(level, (ROWS, VDIM))
    latent = (latent * inverse).astype(BF16)

    small[5].wait()
    pl.semaphore_wait(barrier, SOURCES)

    low = lax.broadcasted_iota(jnp.int32, (BATCH, VDIM), 1) < HALF
    mine = jnp.where(alone, c * ROWS + 4 * ((z - 2 * x) * 8 + y) + x, -1)
    rows = send.reshape(2 * ROWS, VDIM)
    for h in range(HEADS):
        part = jnp.dot(latent[16 * (h // 4) : 16 * (h // 4) + 16], wv[h], preferred_element_type=F32)
        at = 4 * (h % 4)
        rows[pl.ds(4 * h, 4), :] = jnp.where(low, part[at : at + 4], level[4 * h : 4 * h + 4])
        rows[pl.ds(ROWS + 4 * h, 4), :] = jnp.where(low, level[4 * h : 4 * h + 4], part[at : at + 4])
        for b in range(BATCH):
            for core in range(2):
                k = core * ROWS + 4 * h + b
                is_self = mine == k
                pltpu.make_async_remote_copy(
                    src_ref=send.at[k],
                    dst_ref=recv.at[jnp.where(is_self, SOURCES, me)],
                    send_sem=send_sem,
                    recv_sem=recv_sem,
                    device_id=(2 * x + h // 8, h % 8, jnp.where(is_self, 1 - core, core), b),
                    device_id_type=MESH_ID,
                ).start()

    pltpu.make_async_copy(recv.at[pl.ds(0, SOURCES)], recv.at[pl.ds(0, SOURCES)], recv_sem).wait()

    @pl.when(alone)
    def _():
        recv[me] = send[jnp.maximum(mine, 0)]

    gathered = recv.reshape(SOURCES + 1, VDIM)[pl.ds(0, SOURCES), :]
    top = jnp.max(gathered, axis=0, keepdims=True)
    share = pltpu.roll(jnp.exp(gathered - top), HALF, 1)
    result = jnp.sum(share * gathered, axis=0, keepdims=True) / jnp.sum(share, axis=0, keepdims=True)
    out_ref[...] = jnp.where(c == 0, result[:, :HALF], result[:, HALF:]).astype(BF16)
    pltpu.make_async_copy(send, send, send_sem).wait()


def shards(q_nope, q_rope, w_key_up, w_value_up, latent_cache, page_scale, block_table, lengths):
    hbm = pl.BlockSpec(memory_space=pl.ANY)
    dma = pltpu.SemaphoreType.DMA
    return pl.pallas_call(
        kernel,
        out_shape=pltpu.VMEM((1, HALF), BF16),
        in_specs=[hbm] * 8,
        out_specs=pl.BlockSpec(memory_space=pltpu.VMEM),
        scratch_shapes=[
            pltpu.VMEM((BATCH, HEADS, NOPE), BF16),
            pltpu.VMEM((BATCH, HEADS, ROPE), BF16),
            pltpu.VMEM((HEADS, NOPE, LAT), BF16),
            pltpu.VMEM((HEADS, LAT, VDIM), BF16),
            pltpu.VMEM((PAGES, PAGE, LAT + ROPE), BF16),
            pltpu.SMEM((PAGES,), F32),
            pltpu.VMEM((BATCH, BLOCKS), jnp.int32),
            pltpu.SMEM((BATCH,), jnp.int32),
            pltpu.VMEM((ROWS, NOPE), F32),
            pltpu.VMEM((ROWS, ROPE), F32),
            pltpu.VMEM((ROWS, LAT), F32),
            pltpu.VMEM((PAGES * PAGE, ROWS), F32),
            pltpu.VMEM((PAGES, ROWS), F32),
            pltpu.VMEM((2 * ROWS, 1, VDIM), F32),
            pltpu.VMEM((SOURCES + 1, 1, VDIM), F32),
            dma((6,)),
            dma((PIECES,)),
            dma((CHUNKS,)),
            dma,
            dma,
        ],
        compiler_params=pltpu.CompilerParams(collective_id=0, has_side_effects=True),
        name="latent_decode",
    )(q_nope, q_rope, w_key_up, w_value_up, latent_cache, page_scale, block_table, lengths)


def solution(mesh):
    split = Mesh(
        mesh.devices.reshape(8, 8, 2, mesh.shape["head"]), ("seq_0", "seq_1", "seq_2", "head")
    )
    return jax.shard_map(
        shards,
        mesh=split,
        in_specs=(
            P(None, "head", None),
            P(None, "head", None),
            P("head", None, None),
            P("head", None, None),
            P(SEQ, None, None),
            P(SEQ),
            P(None, SEQ),
            P(),
        ),
        out_specs=P("head", SEQ),
        check_vma=False,
    )
```

time: 30.7 us -> 24.5 us (0.80)
  Pallas kernels: 29.3 us -> 23.9 us
  local copies, waits for them, and re-layouts: 1.19 us -> 0.51 us
    pallas_call x1, Pallas kernels: 29.3 us -> 23.9 us  [shards(): pl.pallas_call(kernel, out_shape=pltpu.VMEM((1, HALF), BF16), in_specs=[h...]
    unnamed x1, local copies, waits for them, and re-layouts: 1.19 us -> 0.51 us
where the time goes in v2:
time: 24.5 us; the launch traced here: 24.4 us
  Pallas kernels  23.9 us (98%)
  local copies, waits for them, and re-layouts  0.51 us (2%)
    pallas_call x1, Pallas kernels, shards(): pl.pallas_call(kernel, out_shape=pltpu.VMEM((1, HALF), BF16), in_specs=[h...  23.9 us
    unnamed x1, local copies, waits for them, and re-layouts  0.51 us

profile of v2, /device:TPU:1, one launch (start us, length us, event | category | flops | bytes accessed | tf_op | source)
XLA Modules:
  0.0 24.4 jit_solution(13151968576443665194)
XLA Ops:
  0.0 23.9 %latent_decode.1 = bf16[1,64]{1,0:T(2,128)(2,1)S(1)} custom-call(bf16[4,16,128]{2,1,0:T(8,128)(2,1)} %qn_hbm.1, bf16[4,16,64]{2,1,0:T(8,128)(2,1)} %qr_hbm.1, bf16[16,128,512]{2,1,0:T(8,128)(2,1)} %wk_hbm.1, bf16[16,512,128]{2,1,0:T(8,128)(2,1)} %wv_hbm.1, bf16[64,64,576]{2,1,0:T(8,128)(2,1)} %cache_hbm.1, f32[64]{0:T(128)} %ps_hbm.1, s32[4,16]{1,0:T(4,128)} %bt_hbm.1, ...), custom_call_target="tpu_custom_call" | custom-call | tf_op jit(solution)/shard_map/latent_decode/pallas_call | solution.py:195
  23.9 0.5 %copy.10 = bf16[1,64]{1,0:T(2,128)(2,1)} copy(bf16[1,64]{1,0:T(2,128)(2,1)S(1)} %latent_decode.1) | data formatting | bytes 256

commit v3 on v2

v3 whole, which is shorter than its diff:
```python
import jax
import jax.numpy as jnp
from jax import lax
from jax.experimental import pallas as pl
from jax.experimental.pallas import tpu as pltpu
from jax.sharding import Mesh
from jax.sharding import PartitionSpec as P

SEQ = ("seq_0", "seq_1", "seq_2")
F32 = jnp.float32
BF16 = jnp.bfloat16

BATCH = 4
HEADS = 16
ROWS = BATCH * HEADS
LAT = 512
ROPE = 64
NOPE = 128
VDIM = 128
HALF = VDIM // 2
PAGE = 64
PAGES = 64
BLOCKS = 16
CHUNK = 8
CHUNKS = PAGES // CHUNK
SPAN = CHUNK * PAGE
PIECES = 4
PIECE = HEADS // PIECES
LANES = 128
SIDE = 4
PARTS = 2
TILES = SIDE * ROWS // LANES
NX = 4
EARLY = 6
UNROLL = 8
SOURCES = 128
FLOOR = -1e30


def place(rhs, first, depth, block):
    empty = jnp.zeros((depth, ROWS), BF16)
    left = jnp.concatenate([block, empty], axis=1)
    right = jnp.concatenate([empty, block], axis=1)
    for i in range(SIDE):
        rhs[pl.ds(first + i * depth, depth), pl.ds(i // 2 * LANES, LANES)] = right if i % 2 else left


def kernel(
    qn_hbm, qr_hbm, wk_hbm, wv_hbm, cache_hbm, ps_hbm, bt_hbm, len_hbm, out_ref,
    qn, qr, wk, wv, cache, ps, bt, ln, qs, qrs, ql, s_buf, vc, rhs, send, recv,
    in_sem, wk_sem, cache_sem, send_sem, recv_sem,
):
    z = lax.axis_index("seq_0")
    y = lax.axis_index("seq_1")
    c = lax.axis_index("seq_2")
    x = lax.axis_index("head")

    small = [
        pltpu.make_async_copy(src, dst, in_sem.at[k])
        for k, (src, dst) in enumerate(
            [(qn_hbm, qn), (qr_hbm, qr), (bt_hbm, bt), (len_hbm, ln), (ps_hbm, ps), (wv_hbm, wv)]
        )
    ]
    keys = [
        pltpu.make_async_copy(
            wk_hbm.at[pl.ds(k * PIECE, PIECE)], wk.at[pl.ds(k * PIECE, PIECE)], wk_sem.at[k]
        )
        for k in range(PIECES)
    ]
    pages = [
        pltpu.make_async_copy(
            cache_hbm.at[pl.ds(k * CHUNK, CHUNK)], cache.at[pl.ds(k * CHUNK, CHUNK)], cache_sem.at[k]
        )
        for k in range(CHUNKS)
    ]
    for copy in small[:5] + keys:
        copy.start()

    me = (z * 8 + y) * 2 + c
    plane = lax.div(z, 2)
    alone = plane == x
    other = me + 1 - 2 * c
    barrier = pltpu.get_barrier_semaphore()

    def greet(k):
        pl.semaphore_signal(
            barrier, inc=1, device_id=k * NX + plane, device_id_type=pl.DeviceIdType.LOGICAL
        )

    greet(jnp.where(alone, other, me))

    def greet_all(first, last):
        @pl.loop(first, last)
        def _(i):
            for j in range(1, UNROLL + 1):
                greet(lax.rem(me + i * UNROLL + j, SOURCES))

    greet_all(0, EARLY)
    for copy in pages[:SIDE]:
        copy.start()
    greet_all(EARLY, SOURCES // UNROLL - 1)
    for j in range(1, UNROLL):
        greet(lax.rem(me + SOURCES - UNROLL + j, SOURCES))
    for copy in pages[SIDE:]:
        copy.start()

    for copy in small[:5]:
        copy.wait()
    for b in range(BATCH):
        qs[pl.ds(b, HEADS, stride=BATCH), :] = qn[b].astype(F32)
        qrs[pl.ds(b, HEADS, stride=BATCH), :] = qr[b].astype(F32)

    request = lax.rem(lax.broadcasted_iota(jnp.int32, (PAGES, ROWS), 1), BATCH)
    page_id = lax.broadcasted_iota(jnp.int32, (PAGES, BLOCKS), 0)
    block = lax.broadcasted_iota(jnp.int32, (PAGES, BLOCKS), 1)
    valid = jnp.zeros((PAGES, ROWS), F32)
    for b in range(BATCH):
        left = jnp.clip(ln[b] - (me * BLOCKS + block) * PAGE, 0, PAGE).astype(F32)
        owned = jnp.where(jnp.broadcast_to(bt[b : b + 1, :], (PAGES, BLOCKS)) == page_id, left, 0.0)
        valid = jnp.where(request == b, jnp.sum(owned, axis=1, keepdims=True), valid)
    for g in range(PAGES // 16):
        vc[g] = jnp.concatenate([valid[16 * g : 16 * g + 8], valid[16 * g + 8 : 16 * g + 16]], axis=1)
    rhs[...] = jnp.zeros((SIDE * (LAT + ROPE), SIDE * ROWS), BF16)
    place(rhs, SIDE * LAT, ROPE, qrs[...].T.astype(BF16))

    for k in range(PIECES):
        keys[k].wait()
        for h in range(k * PIECE, (k + 1) * PIECE):
            lhs = qs[pl.ds(16 * (h // 4), 16), :].astype(BF16)
            part = jnp.dot(lhs, wk[h], preferred_element_type=F32)
            at = 4 * (h % 4)
            ql[pl.ds(4 * h, 4), :] = part[at : at + 4]
    place(rhs, 0, LAT, ql[...].T.astype(BF16))

    small[5].start()
    row_id = lax.broadcasted_iota(jnp.int32, (PAGE, LANES), 0).astype(F32)
    even = lax.broadcasted_iota(jnp.int32, (1, LANES), 1) < ROWS

    def scale_of(s, tile, page):
        p = (s * SIDE + 2 * tile) * CHUNK + page
        return jnp.where(even, ps[p], ps[p + CHUNK])

    def scores(s):
        for i in range(SIDE):
            pages[s * SIDE + i].wait()
        raw = []
        for part in range(PARTS):
            first = part * (CHUNK // PARTS)
            here = [pl.ds((s * SIDE + i) * CHUNK + first, CHUNK // PARTS) for i in range(SIDE)]
            lhs = [cache[at, :, :LAT].reshape(SPAN // PARTS, LAT) for at in here]
            lhs = lhs + [cache[at, :, LAT:].reshape(SPAN // PARTS, ROPE) for at in here]
            raw.append(jnp.dot(jnp.concatenate(lhs, axis=1), rhs[...], preferred_element_type=F32))
        peak = jnp.full((PAGE, LANES), FLOOR, F32)
        for page in range(CHUNK):
            for tile in range(TILES):
                scale = scale_of(s, tile, page) * (NOPE + ROPE) ** (-0.5)
                at = page % (CHUNK // PARTS) * PAGE
                scaled = raw[page // (CHUNK // PARTS)][at : at + PAGE, tile * LANES : (tile + 1) * LANES] * scale
                score = jnp.where(row_id < vc[s * TILES + tile, pl.ds(page, 1), :], scaled, FLOOR)
                s_buf[s, tile, pl.ds(page * PAGE, PAGE), :] = score
                peak = jnp.maximum(peak, score)
        peak = jnp.max(peak, axis=0, keepdims=True)
        return jnp.maximum(peak, pltpu.roll(peak, ROWS, 1))

    def weighted(s, floor):
        total = jnp.zeros((PAGE, LANES), F32)
        latent = [jnp.zeros((ROWS, LAT // PARTS), F32) for _ in range(PARTS)]
        for tile in range(TILES):
            pieces = []
            for page in range(CHUNK):
                weight = jnp.exp(s_buf[s, tile, pl.ds(page * PAGE, PAGE), :] - floor)
                total = total + weight
                pieces.append(weight * scale_of(s, tile, page))
            prob = jnp.concatenate(pieces, axis=0).T.astype(BF16)
            for i in range(2):
                k = s * SIDE + 2 * tile + i
                for part in range(PARTS):
                    columns = pl.ds(part * (LAT // PARTS), LAT // PARTS)
                    lat_rows = cache[pl.ds(k * CHUNK, CHUNK), :, columns].reshape(SPAN, LAT // PARTS)
                    latent[part] = latent[part] + jnp.dot(
                        prob[i * ROWS : (i + 1) * ROWS], lat_rows, preferred_element_type=F32
                    )
        total = jnp.sum(total, axis=0, keepdims=True)
        return total + pltpu.roll(total, ROWS, 1), jnp.concatenate(latent, axis=1)

    former = jnp.maximum(scores(0), -1e29)
    floor = jnp.maximum(scores(1), former)
    total, latent = weighted(0, former)
    total_two, latent_two = weighted(1, floor)
    correction = jnp.exp(former - floor)
    denominator = total * correction + total_two

    some = denominator > 0.0
    safe = jnp.where(some, denominator, 1.0)
    level = jnp.where(some, floor + jnp.log(safe), FLOOR)
    sub = lax.broadcasted_iota(jnp.int32, (8, LANES), 0)
    inverse = 1.0 / safe
    columns = jnp.where(sub == 0, level, jnp.where(sub == 1, inverse, correction * inverse)).T
    level = jnp.broadcast_to(columns[:ROWS, 0:1], (ROWS, VDIM))
    latent = (latent * columns[:ROWS, 2:3] + latent_two * columns[:ROWS, 1:2]).astype(BF16)

    small[5].wait()
    pl.semaphore_wait(barrier, SOURCES)
    sub = lax.broadcasted_iota(jnp.int32, (8, VDIM), 0)
    low = lax.broadcasted_iota(jnp.int32, (8, VDIM), 1) < HALF
    data_lane = (sub < BATCH) == low
    rows = send.reshape(2 * ROWS, VDIM)
    mine = lax.rem(me * NX + x, SOURCES)

    def post(t, slot, to):
        pltpu.make_async_remote_copy(
            src_ref=send.at[t],
            dst_ref=recv.at[slot],
            send_sem=send_sem,
            recv_sem=recv_sem,
            device_id=to,
            device_id_type=pl.DeviceIdType.LOGICAL,
        ).start()

    def project(h):
        part = jnp.dot(latent[16 * (h // 4) : 16 * (h // 4) + 16], wv[h], preferred_element_type=F32)
        at = 4 * (h % 4)
        part = part[at : at + 4]
        mark = level[4 * h : 4 * h + 4]
        rows[pl.ds(8 * h, 8), :] = jnp.where(
            data_lane, jnp.concatenate([part, part], axis=0), jnp.concatenate([mark, mark], axis=0)
        )

    project(0)
    for t in range(8):
        is_self = jnp.logical_and(alone, mine == t)
        post(t, jnp.where(is_self, SOURCES, me), SOURCES * x + jnp.where(is_self, t ^ NX, t))
    for h in range(1, HEADS):
        project(h)

    @pl.loop(1, SOURCES // UNROLL)
    def _(i):
        for j in range(UNROLL):
            t = i * UNROLL + j
            is_self = jnp.logical_and(alone, mine == t)
            turned = SOURCES * x + t + jnp.where(is_self, NX * (1 - 2 * c), 0)
            post(t, jnp.where(is_self, SOURCES, me), turned)

    pltpu.make_async_copy(recv.at[pl.ds(0, SOURCES)], recv.at[pl.ds(0, SOURCES)], recv_sem).wait()

    @pl.when(alone)
    def _():
        recv[me] = send[mine]

    gathered = recv.reshape(SOURCES + 1, VDIM)[pl.ds(0, SOURCES), :]
    top = jnp.max(gathered, axis=0, keepdims=True)
    share = pltpu.roll(jnp.exp(gathered - top), HALF, 1)
    result = jnp.sum(share * gathered, axis=0, keepdims=True) / jnp.sum(share, axis=0, keepdims=True)
    out_ref[...] = jnp.where(c == 0, result[:, :HALF], result[:, HALF:]).astype(BF16)
    pltpu.make_async_copy(send, send, send_sem).wait()


def shards(q_nope, q_rope, w_key_up, w_value_up, latent_cache, page_scale, block_table, lengths):
    hbm = pl.BlockSpec(memory_space=pl.ANY)
    dma = pltpu.SemaphoreType.DMA
    return pl.pallas_call(
        kernel,
        out_shape=pltpu.VMEM((1, HALF), BF16),
        in_specs=[hbm] * 8,
        out_specs=pl.BlockSpec(memory_space=pltpu.VMEM),
        scratch_shapes=[
            pltpu.VMEM((BATCH, HEADS, NOPE), BF16),
            pltpu.VMEM((BATCH, HEADS, ROPE), BF16),
            pltpu.VMEM((HEADS, NOPE, LAT), BF16),
            pltpu.VMEM((HEADS, LAT, VDIM), BF16),
            pltpu.VMEM((PAGES, PAGE, LAT + ROPE), BF16),
            pltpu.SMEM((PAGES,), F32),
            pltpu.VMEM((BATCH, BLOCKS), jnp.int32),
            pltpu.SMEM((BATCH,), jnp.int32),
            pltpu.VMEM((ROWS, NOPE), F32),
            pltpu.VMEM((ROWS, ROPE), F32),
            pltpu.VMEM((ROWS, LAT), F32),
            pltpu.VMEM((CHUNKS // SIDE, TILES, SPAN, LANES), F32),
            pltpu.VMEM((PAGES // 16, 8, LANES), F32),
            pltpu.VMEM((SIDE * (LAT + ROPE), SIDE * ROWS), BF16),
            pltpu.VMEM((2 * ROWS, 1, VDIM), F32),
            pltpu.VMEM((SOURCES + 1, 1, VDIM), F32),
            dma((6,)),
            dma((PIECES,)),
            dma((CHUNKS,)),
            dma,
            dma,
        ],
        compiler_params=pltpu.CompilerParams(collective_id=0, has_side_effects=True),
        name="latent_decode",
    )(q_nope, q_rope, w_key_up, w_value_up, latent_cache, page_scale, block_table, lengths)


def solution(mesh):
    split = Mesh(
        mesh.devices.reshape(8, 8, 2, mesh.shape["head"]), ("seq_0", "seq_1", "seq_2", "head")
    )
    return jax.shard_map(
        shards,
        mesh=split,
        in_specs=(
            P(None, "head", None),
            P(None, "head", None),
            P("head", None, None),
            P("head", None, None),
            P(SEQ, None, None),
            P(SEQ),
            P(None, SEQ),
            P(),
        ),
        out_specs=P("head", SEQ),
        check_vma=False,
    )
```

time: 24.5 us -> 23.8 us (0.971)
  Pallas kernels: 23.9 us -> 23.2 us
    pallas_call x1, Pallas kernels: 23.9 us -> 23.2 us  [shards(): pl.pallas_call(kernel, out_shape=pltpu.VMEM((1, HALF), BF16), in_specs=[h...]
where the time goes in v3:
time: 23.8 us; the launch traced here: 23.7 us
  Pallas kernels  23.2 us (97%)
  local copies, waits for them, and re-layouts  0.51 us (2%)
    pallas_call x1, Pallas kernels, shards(): pl.pallas_call(kernel, out_shape=pltpu.VMEM((1, HALF), BF16), in_specs=[h...  23.2 us
    unnamed x1, local copies, waits for them, and re-layouts  0.51 us

profile of v3, /device:TPU:1, one launch (start us, length us, event | category | flops | bytes accessed | tf_op | source)
XLA Modules:
  0.0 23.7 jit_solution(10538974905736890629)
XLA Ops:
  0.0 23.2 %latent_decode.1 = bf16[1,64]{1,0:T(2,128)(2,1)S(1)} custom-call(bf16[4,16,128]{2,1,0:T(8,128)(2,1)} %qn_hbm.1, bf16[4,16,64]{2,1,0:T(8,128)(2,1)} %qr_hbm.1, bf16[16,128,512]{2,1,0:T(8,128)(2,1)} %wk_hbm.1, bf16[16,512,128]{2,1,0:T(8,128)(2,1)} %wv_hbm.1, bf16[64,64,576]{2,1,0:T(8,128)(2,1)} %cache_hbm.1, f32[64]{0:T(128)} %ps_hbm.1, s32[4,16]{1,0:T(4,128)} %bt_hbm.1, ...), custom_call_target="tpu_custom_call" | custom-call | tf_op jit(solution)/shard_map/latent_decode/pallas_call | solution.py:261
  23.2 0.5 %copy.10 = bf16[1,64]{1,0:T(2,128)(2,1)} copy(bf16[1,64]{1,0:T(2,128)(2,1)S(1)} %latent_decode.1) | data formatting | bytes 256

commit v4 on v3

--- a/solution.py
+++ b/solution.py
@@ -31,7 +31,8 @@
 PARTS = 2
 TILES = SIDE * ROWS // LANES
 NX = 4
-EARLY = 6
+EARLY = 4
+LATE = 11
 UNROLL = 8
 SOURCES = 128
 FLOOR = -1e30
@@ -76,6 +77,8 @@
     for copy in small[:5] + keys:
         copy.start()
 
+    rhs[...] = jnp.zeros((SIDE * (LAT + ROPE), SIDE * ROWS), BF16)
+
     me = (z * 8 + y) * 2 + c
     plane = lax.div(z, 2)
     alone = plane == x
@@ -98,13 +101,14 @@
     greet_all(0, EARLY)
     for copy in pages[:SIDE]:
         copy.start()
-    greet_all(EARLY, SOURCES // UNROLL - 1)
+    greet_all(EARLY, LATE)
+    for copy in pages[SIDE:]:
+        copy.start()
+    greet_all(LATE, SOURCES // UNROLL - 1)
     for j in range(1, UNROLL):
         greet(lax.rem(me + SOURCES - UNROLL + j, SOURCES))
-    for copy in pages[SIDE:]:
-        copy.start()
-
-    for copy in small[:5]:
+
+    for copy in small[:5] + keys:
         copy.wait()
     for b in range(BATCH):
         qs[pl.ds(b, HEADS, stride=BATCH), :] = qn[b].astype(F32)
@@ -120,16 +124,13 @@
         valid = jnp.where(request == b, jnp.sum(owned, axis=1, keepdims=True), valid)
     for g in range(PAGES // 16):
         vc[g] = jnp.concatenate([valid[16 * g : 16 * g + 8], valid[16 * g + 8 : 16 * g + 16]], axis=1)
-    rhs[...] = jnp.zeros((SIDE * (LAT + ROPE), SIDE * ROWS), BF16)
     place(rhs, SIDE * LAT, ROPE, qrs[...].T.astype(BF16))
 
-    for k in range(PIECES):
-        keys[k].wait()
-        for h in range(k * PIECE, (k + 1) * PIECE):
-            lhs = qs[pl.ds(16 * (h // 4), 16), :].astype(BF16)
-            part = jnp.dot(lhs, wk[h], preferred_element_type=F32)
-            at = 4 * (h % 4)
-            ql[pl.ds(4 * h, 4), :] = part[at : at + 4]
+    for h in range(HEADS):
+        lhs = qs[pl.ds(16 * (h // 4), 16), :].astype(BF16)
+        part = jnp.dot(lhs, wk[h], preferred_element_type=F32)
+        at = 4 * (h % 4)
+        ql[pl.ds(4 * h, 4), :] = part[at : at + 4]
     place(rhs, 0, LAT, ql[...].T.astype(BF16))
 
     small[5].start()
@@ -140,7 +141,7 @@
         p = (s * SIDE + 2 * tile) * CHUNK + page
         return jnp.where(even, ps[p], ps[p + CHUNK])
 
-    def scores(s):
+    def products(s):
         for i in range(SIDE):
             pages[s * SIDE + i].wait()
         raw = []
@@ -150,6 +151,9 @@
             lhs = [cache[at, :, :LAT].reshape(SPAN // PARTS, LAT) for at in here]
             lhs = lhs + [cache[at, :, LAT:].reshape(SPAN // PARTS, ROPE) for at in here]
             raw.append(jnp.dot(jnp.concatenate(lhs, axis=1), rhs[...], preferred_element_type=F32))
+        return raw
+
+    def scores(s, raw):
         peak = jnp.full((PAGE, LANES), FLOOR, F32)
         for page in range(CHUNK):
             for tile in range(TILES):
@@ -183,8 +187,9 @@
         total = jnp.sum(total, axis=0, keepdims=True)
         return total + pltpu.roll(total, ROWS, 1), jnp.concatenate(latent, axis=1)
 
-    former = jnp.maximum(scores(0), -1e29)
-    floor = jnp.maximum(scores(1), former)
+    raw = [products(s) for s in range(CHUNKS // SIDE)]
+    former = jnp.maximum(scores(0, raw[0]), -1e29)
+    floor = jnp.maximum(scores(1, raw[1]), former)
     total, latent = weighted(0, former)
     total_two, latent_two = weighted(1, floor)
     correction = jnp.exp(former - floor)
@@ -241,17 +246,19 @@
             turned = SOURCES * x + t + jnp.where(is_self, NX * (1 - 2 * c), 0)
             post(t, jnp.where(is_self, SOURCES, me), turned)
 
-    pltpu.make_async_copy(recv.at[pl.ds(0, SOURCES)], recv.at[pl.ds(0, SOURCES)], recv_sem).wait()
-
     @pl.when(alone)
     def _():
         recv[me] = send[mine]
 
+    pltpu.make_async_copy(recv.at[pl.ds(0, SOURCES)], recv.at[pl.ds(0, SOURCES)], recv_sem).wait()
+
     gathered = recv.reshape(SOURCES + 1, VDIM)[pl.ds(0, SOURCES), :]
-    top = jnp.max(gathered, axis=0, keepdims=True)
-    share = pltpu.roll(jnp.exp(gathered - top), HALF, 1)
-    result = jnp.sum(share * gathered, axis=0, keepdims=True) / jnp.sum(share, axis=0, keepdims=True)
-    out_ref[...] = jnp.where(c == 0, result[:, :HALF], result[:, HALF:]).astype(BF16)
+    turned = pltpu.roll(gathered, HALF, 1)
+    marks = jnp.where(c == 0, turned, gathered)
+    share = jnp.exp(marks - jnp.max(marks, axis=0, keepdims=True))
+    share_of = share * jnp.where(c == 0, gathered, turned)
+    result = jnp.sum(share_of, axis=0, keepdims=True) / jnp.sum(share, axis=0, keepdims=True)
+    out_ref[...] = result[:, :HALF].astype(BF16)
     pltpu.make_async_copy(send, send, send_sem).wait()
 
 

time: 23.8 us -> 23.5 us (0.987)
  Pallas kernels: 23.2 us -> 22.9 us
    pallas_call x1, Pallas kernels: 23.2 us -> 22.9 us  [shards(): pl.pallas_call(kernel, out_shape=pltpu.VMEM((1, HALF), BF16), in_specs=[h...]
where the time goes in v4:
time: 23.5 us; the launch traced here: 23.4 us
  Pallas kernels  22.9 us (97%)
  local copies, waits for them, and re-layouts  0.51 us (2%)
    pallas_call x1, Pallas kernels, shards(): pl.pallas_call(kernel, out_shape=pltpu.VMEM((1, HALF), BF16), in_specs=[h...  22.9 us
    unnamed x1, local copies, waits for them, and re-layouts  0.51 us

profile of v4, /device:TPU:1, one launch (start us, length us, event | category | flops | bytes accessed | tf_op | source)
XLA Modules:
  0.0 23.4 jit_solution(15304596987181560257)
XLA Ops:
  0.0 22.9 %latent_decode.1 = bf16[1,64]{1,0:T(2,128)(2,1)S(1)} custom-call(bf16[4,16,128]{2,1,0:T(8,128)(2,1)} %qn_hbm.1, bf16[4,16,64]{2,1,0:T(8,128)(2,1)} %qr_hbm.1, bf16[16,128,512]{2,1,0:T(8,128)(2,1)} %wk_hbm.1, bf16[16,512,128]{2,1,0:T(8,128)(2,1)} %wv_hbm.1, bf16[64,64,576]{2,1,0:T(8,128)(2,1)} %cache_hbm.1, f32[64]{0:T(128)} %ps_hbm.1, s32[4,16]{1,0:T(4,128)} %bt_hbm.1, ...), custom_call_target="tpu_custom_call" | custom-call | tf_op jit(solution)/shard_map/latent_decode/pallas_call | solution.py:268
  22.9 0.5 %copy.10 = bf16[1,64]{1,0:T(2,128)(2,1)} copy(bf16[1,64]{1,0:T(2,128)(2,1)S(1)} %latent_decode.1) | data formatting | bytes 256

commit v5 on v4

--- a/solution.py
+++ b/solution.py
@@ -29,7 +29,7 @@
 LANES = 128
 SIDE = 4
 PARTS = 2
-TILES = SIDE * ROWS // LANES
+TILES = 2
 NX = 4
 EARLY = 4
 LATE = 11
@@ -40,10 +40,8 @@
 
 def place(rhs, first, depth, block):
     empty = jnp.zeros((depth, ROWS), BF16)
-    left = jnp.concatenate([block, empty], axis=1)
-    right = jnp.concatenate([empty, block], axis=1)
-    for i in range(SIDE):
-        rhs[pl.ds(first + i * depth, depth), pl.ds(i // 2 * LANES, LANES)] = right if i % 2 else left
+    rhs[pl.ds(first, depth), :] = jnp.concatenate([block, empty], axis=1)
+    rhs[pl.ds(first + depth, depth), :] = jnp.concatenate([empty, block], axis=1)
 
 
 def kernel(
@@ -76,8 +74,6 @@
     ]
     for copy in small[:5] + keys:
         copy.start()
-
-    rhs[...] = jnp.zeros((SIDE * (LAT + ROPE), SIDE * ROWS), BF16)
 
     me = (z * 8 + y) * 2 + c
     plane = lax.div(z, 2)
@@ -124,7 +120,7 @@
         valid = jnp.where(request == b, jnp.sum(owned, axis=1, keepdims=True), valid)
     for g in range(PAGES // 16):
         vc[g] = jnp.concatenate([valid[16 * g : 16 * g + 8], valid[16 * g + 8 : 16 * g + 16]], axis=1)
-    place(rhs, SIDE * LAT, ROPE, qrs[...].T.astype(BF16))
+    place(rhs, 2 * LAT, ROPE, qrs[...].T.astype(BF16))
 
     for h in range(HEADS):
         lhs = qs[pl.ds(16 * (h // 4), 16), :].astype(BF16)
@@ -145,12 +141,15 @@
         for i in range(SIDE):
             pages[s * SIDE + i].wait()
         raw = []
-        for part in range(PARTS):
-            first = part * (CHUNK // PARTS)
-            here = [pl.ds((s * SIDE + i) * CHUNK + first, CHUNK // PARTS) for i in range(SIDE)]
-            lhs = [cache[at, :, :LAT].reshape(SPAN // PARTS, LAT) for at in here]
-            lhs = lhs + [cache[at, :, LAT:].reshape(SPAN // PARTS, ROPE) for at in here]
-            raw.append(jnp.dot(jnp.concatenate(lhs, axis=1), rhs[...], preferred_element_type=F32))
+        for tile in range(TILES):
+            here = [pl.ds((s * SIDE + 2 * tile + i) * CHUNK, CHUNK) for i in range(2)]
+            lhs = [cache[at, :, :LAT].reshape(SPAN, LAT) for at in here]
+            lhs = lhs + [cache[at, :, LAT:].reshape(SPAN, ROPE) for at in here]
+            lhs = jnp.concatenate(lhs, axis=1)
+            halves = [lhs[: SPAN // 2], lhs[SPAN // 2 :]]
+            raw.append(
+                jnp.concatenate([jnp.dot(m, rhs[...], preferred_element_type=F32) for m in halves], axis=0)
+            )
         return raw
 
     def scores(s, raw):
@@ -158,8 +157,7 @@
         for page in range(CHUNK):
             for tile in range(TILES):
                 scale = scale_of(s, tile, page) * (NOPE + ROPE) ** (-0.5)
-                at = page % (CHUNK // PARTS) * PAGE
-                scaled = raw[page // (CHUNK // PARTS)][at : at + PAGE, tile * LANES : (tile + 1) * LANES] * scale
+                scaled = raw[tile][page * PAGE : (page + 1) * PAGE] * scale
                 score = jnp.where(row_id < vc[s * TILES + tile, pl.ds(page, 1), :], scaled, FLOOR)
                 s_buf[s, tile, pl.ds(page * PAGE, PAGE), :] = score
                 peak = jnp.maximum(peak, score)
@@ -232,7 +230,7 @@
         )
 
     project(0)
-    for t in range(8):
+    for t in (4, 5, 6, 7, 0, 1, 2, 3):
         is_self = jnp.logical_and(alone, mine == t)
         post(t, jnp.where(is_self, SOURCES, me), SOURCES * x + jnp.where(is_self, t ^ NX, t))
     for h in range(1, HEADS):
@@ -284,7 +282,7 @@
             pltpu.VMEM((ROWS, LAT), F32),
             pltpu.VMEM((CHUNKS // SIDE, TILES, SPAN, LANES), F32),
             pltpu.VMEM((PAGES // 16, 8, LANES), F32),
-            pltpu.VMEM((SIDE * (LAT + ROPE), SIDE * ROWS), BF16),
+            pltpu.VMEM((2 * (LAT + ROPE), LANES), BF16),
             pltpu.VMEM((2 * ROWS, 1, VDIM), F32),
             pltpu.VMEM((SOURCES + 1, 1, VDIM), F32),
             dma((6,)),

time: 23.5 us -> 23.4 us (level)
  no operation moved by 1% of the time
where the time goes in v5:
time: 23.4 us; the launch traced here: 23.3 us
  Pallas kernels  22.7 us (97%)
  local copies, waits for them, and re-layouts  0.51 us (2%)
    pallas_call x1, Pallas kernels, shards(): pl.pallas_call(kernel, out_shape=pltpu.VMEM((1, HALF), BF16), in_specs=[h...  22.7 us
    unnamed x1, local copies, waits for them, and re-layouts  0.51 us

profile of v5, /device:TPU:1, one launch (start us, length us, event | category | flops | bytes accessed | tf_op | source)
XLA Modules:
  0.0 23.3 jit_solution(12144374295314490972)
XLA Ops:
  0.0 22.7 %latent_decode.1 = bf16[1,64]{1,0:T(2,128)(2,1)S(1)} custom-call(bf16[4,16,128]{2,1,0:T(8,128)(2,1)} %qn_hbm.1, bf16[4,16,64]{2,1,0:T(8,128)(2,1)} %qr_hbm.1, bf16[16,128,512]{2,1,0:T(8,128)(2,1)} %wk_hbm.1, bf16[16,512,128]{2,1,0:T(8,128)(2,1)} %wv_hbm.1, bf16[64,64,576]{2,1,0:T(8,128)(2,1)} %cache_hbm.1, f32[64]{0:T(128)} %ps_hbm.1, s32[4,16]{1,0:T(4,128)} %bt_hbm.1, ...), custom_call_target="tpu_custom_call" | custom-call | tf_op jit(solution)/shard_map/latent_decode/pallas_call | solution.py:266
  22.7 0.5 %copy.10 = bf16[1,64]{1,0:T(2,128)(2,1)} copy(bf16[1,64]{1,0:T(2,128)(2,1)S(1)} %latent_decode.1) | data formatting | bytes 256

commit v6 on v5

--- a/solution.py
+++ b/solution.py
@@ -31,8 +31,8 @@
 PARTS = 2
 TILES = 2
 NX = 4
-EARLY = 4
-LATE = 11
+EARLY = 2
+LATE = 8
 UNROLL = 8
 SOURCES = 128
 FLOOR = -1e30
@@ -120,7 +120,7 @@
         valid = jnp.where(request == b, jnp.sum(owned, axis=1, keepdims=True), valid)
     for g in range(PAGES // 16):
         vc[g] = jnp.concatenate([valid[16 * g : 16 * g + 8], valid[16 * g + 8 : 16 * g + 16]], axis=1)
-    place(rhs, 2 * LAT, ROPE, qrs[...].T.astype(BF16))
+    place(rhs, 2 * LAT, ROPE, qrs[pl.ds(0, ROWS), :].T.astype(BF16))
 
     for h in range(HEADS):
         lhs = qs[pl.ds(16 * (h // 4), 16), :].astype(BF16)
@@ -277,8 +277,8 @@
             pltpu.SMEM((PAGES,), F32),
             pltpu.VMEM((BATCH, BLOCKS), jnp.int32),
             pltpu.SMEM((BATCH,), jnp.int32),
-            pltpu.VMEM((ROWS, NOPE), F32),
-            pltpu.VMEM((ROWS, ROPE), F32),
+            pltpu.VMEM((ROWS + 8, NOPE), F32),
+            pltpu.VMEM((ROWS + 8, ROPE), F32),
             pltpu.VMEM((ROWS, LAT), F32),
             pltpu.VMEM((CHUNKS // SIDE, TILES, SPAN, LANES), F32),
             pltpu.VMEM((PAGES // 16, 8, LANES), F32),

time: 23.4 us -> 23.3 us (level)
  no operation moved by 1% of the time
where the time goes in v6:
time: 23.3 us; the launch traced here: 23.2 us
  Pallas kernels  22.7 us (97%)
  local copies, waits for them, and re-layouts  0.51 us (2%)
    pallas_call x1, Pallas kernels, shards(): pl.pallas_call(kernel, out_shape=pltpu.VMEM((1, HALF), BF16), in_specs=[h...  22.7 us
    unnamed x1, local copies, waits for them, and re-layouts  0.51 us

profile of v6, /device:TPU:1, one launch (start us, length us, event | category | flops | bytes accessed | tf_op | source)
XLA Modules:
  0.0 23.2 jit_solution(5685643051212874227)
XLA Ops:
  0.0 22.7 %latent_decode.1 = bf16[1,64]{1,0:T(2,128)(2,1)S(1)} custom-call(bf16[4,16,128]{2,1,0:T(8,128)(2,1)} %qn_hbm.1, bf16[4,16,64]{2,1,0:T(8,128)(2,1)} %qr_hbm.1, bf16[16,128,512]{2,1,0:T(8,128)(2,1)} %wk_hbm.1, bf16[16,512,128]{2,1,0:T(8,128)(2,1)} %wv_hbm.1, bf16[64,64,576]{2,1,0:T(8,128)(2,1)} %cache_hbm.1, f32[64]{0:T(128)} %ps_hbm.1, s32[4,16]{1,0:T(4,128)} %bt_hbm.1, ...), custom_call_target="tpu_custom_call" | custom-call | tf_op jit(solution)/shard_map/latent_decode/pallas_call | solution.py:266
  22.7 0.5 %copy.10 = bf16[1,64]{1,0:T(2,128)(2,1)} copy(bf16[1,64]{1,0:T(2,128)(2,1)S(1)} %latent_decode.1) | data formatting | bytes 256
